TPU v7x, 256 devices: a 2x2x32 block of a 4x8x32 slice. The times are simulated.
256 devices in a mesh: cohort: 4 (over x, y), tile: 64 (over z, core).
Axes of the slice: x: 2, y: 2, z: 32, core: 2. Of those that a mesh axis runs over, the one named last changes fastest.
The devices are a block of a 4x8x32 slice.
Arguments:
- dosage: bfloat16 [4096, 8192], P(('cohort', 'tile')), parts along dimension 0, may hold values from 0 to 2
- covars: float32 [4096, 16], P(('cohort', 'tile')), parts along dimension 0, may hold values from -12 to 12, as said below
- phenotypes: float32 [4096, 7168], P(('cohort', 'tile')), parts along dimension 0, may hold values from -100 to 100
Outputs:
- mean_chi: float32 [28672], P(('cohort', 'tile')), parts along dimension 0
- hit_rate: float32 [28672], P(('cohort', 'tile')), parts along dimension 0
There are 4 independent parts, one for each index of `cohort`. A program takes and returns all parts, laid end to end along the dimension named above; each array names one. Nothing has to cross between parts.
Inputs may be any that keep to these rules, and one draw needn't show every extreme that they name: `covars`: each covariate column has its own mean and spread.
All inputs are finite; a program needn't handle non-finite values.
Results may differ from a plain program's by a relative error of at most 0.003.
Values may be sent and summed in bfloat16 or wider, within the bound.
A program may use at most 64 MiB of HBM per device.

v0:
```python
import jax
import jax.numpy as jnp
from jax import lax
from jax.sharding import Mesh
from jax.sharding import PartitionSpec as P

TILE = ("tile_0", "tile_1")
COHORT_TILE = ("cohort", "tile_0", "tile_1")


def in_order(parts, dim):
    shape = list(parts.shape[1:])
    shape[dim] *= parts.shape[0]
    return jnp.moveaxis(parts, 0, dim).reshape(shape)


def gather_in_order(shard, axes, turns):
    parts = shard
    for k in turns:
        parts = lax.all_gather(parts, axes[k])
    done = turns[::-1]
    back = [done.index(k) for k in range(len(axes))]
    parts = parts.transpose(*back, *range(len(axes), parts.ndim))
    return parts.reshape(-1, *shard.shape)


def whole_of(shard, axes, turns, dim):
    return in_order(gather_in_order(shard, axes, turns), dim)


def local(dosage, covars, phenotypes):
    highest = lax.Precision.HIGHEST
    devices = lax.axis_size(TILE)
    local_rows = dosage.shape[0]
    variants = dosage.shape[1]
    samples = local_rows * devices
    genes_all = phenotypes.shape[1]
    gene_own = genes_all // devices
    scale_root = jnp.sqrt(jnp.float32(samples))
    covars_all = whole_of(covars, TILE, (0, 1), 0)
    dose_all = lax.all_gather(dosage, TILE, axis=0, tiled=True)
    pheno_own = lax.all_to_all(phenotypes, TILE, split_axis=1, concat_axis=0, tiled=True)
    gram = jnp.dot(covars_all.T, covars_all, precision=highest, preferred_element_type=jnp.float32)
    factor = jnp.linalg.cholesky(gram)
    cov_pheno = jnp.dot(
        covars_all.T, pheno_own, precision=highest, preferred_element_type=jnp.float32
    )
    beta_pheno = jax.scipy.linalg.cho_solve((factor, True), cov_pheno)
    pheno_resid = pheno_own - jnp.dot(
        covars_all, beta_pheno, precision=highest, preferred_element_type=jnp.float32
    )
    pheno_sumsq = jnp.sum(pheno_resid * pheno_resid, axis=0)
    pheno_bf = pheno_resid.astype(jnp.bfloat16)
    pheno_var = pheno_sumsq / samples + 0.1
    width = 1024
    blocks = variants // width

    def one_block(index, totals):
        start = index * width
        dose_block = lax.dynamic_slice_in_dim(dose_all, start, width, 1).astype(jnp.float32)
        cov_dose = jnp.dot(
            covars_all.T, dose_block, precision=highest, preferred_element_type=jnp.float32
        )
        beta_dose = jax.scipy.linalg.cho_solve((factor, True), cov_dose)
        dose_resid = dose_block - jnp.dot(
            covars_all, beta_dose, precision=highest, preferred_element_type=jnp.float32
        )
        dose_var = jnp.sum(dose_resid * dose_resid, axis=0) / samples + 0.1
        cross = lax.dot_general(
            pheno_bf,
            dose_resid.astype(jnp.bfloat16),
            (((0,), (0,)), ((), ())),
            preferred_element_type=jnp.float32,
        )
        zscore = cross / (scale_root * jnp.sqrt(pheno_var[:, None] * dose_var[None, :]))
        chi_square = zscore * zscore
        return (
            totals[0] + jnp.sum(chi_square, axis=1),
            totals[1] + jnp.sum(jax.nn.sigmoid(2.0 * (chi_square - 4.0)), axis=1),
        )

    zeros = jnp.zeros((gene_own,), jnp.float32)
    chi_total, hit_total = lax.fori_loop(0, blocks, one_block, (zeros, zeros))
    return (chi_total / variants, 20.0 / variants * hit_total)


def solution(mesh):
    finer = Mesh(mesh.devices.reshape(mesh.shape["cohort"], 32, 2), ("cohort", "tile_0", "tile_1"))
    return jax.shard_map(
        local,
        mesh=finer,
        in_specs=(P(COHORT_TILE, None), P(COHORT_TILE, None), P(COHORT_TILE, None)),
        out_specs=(P(COHORT_TILE), P(COHORT_TILE)),
        check_vma=False,
    )
```

profile of v0, /device:TPU:37, one launch (start us, length us, event | category | flops | bytes accessed | tf_op | source)
XLA Modules:
  0.0 319.9 jit_solution(15411580369733609212)
XLA Ops:
  7.2 0.7 all-gather.4.cloned.1.call-update
  8.0 1.3 all_to_all.14
  9.3 1.1 copy.19
  10.4 34.3 %all-to-all-start = ((f32[16,64,112]{2,0,1:T(8,128)}), f32[16,64,112]{2,0,1:T(8,128)S(1)}, u32[]{:S(2)}, u32[]{:S(2)}) async-start(f32[16,64,112]{2,0,1:T(8,128)} %copy.19), calls=%async_computation | async-start | bytes 1048576 | tf_op jit(solution)/shard_map/all_to_all | solution.py:42
  44.8 96.4 %all-gather = f32[512,16]{1,0:T(8,128)S(1)} all-gather(f32[16,16]{1,0:T(8,128)} %param.6), channel_id=2, replica_groups=mesh['cohort'=4,'tile_0'=32,'tile_1'=2] {'tile_0'}, dimensions={0}, use_global_device_ids=true | all-gather | bytes 33792 | tf_op jit(solution)/shard_map/all_gather | solution.py:20
  141.2 9.8 %all-gather.1 = f32[64,16,16]{2,1,0:T(8,128)S(1)} all-gather(f32[32,16,16]{2,1,0:T(8,128)S(1)} %bitcast.97), channel_id=3, replica_groups=mesh['cohort'=4,'tile_0'=32,'tile_1'=2] {'tile_1'}, dimensions={0}, use_global_device_ids=true | all-gather | bytes 98304 | tf_op jit(solution)/shard_map/all_gather | solution.py:20
  151.0 0.2 copy.16
  151.2 0.5 convolution_bitcast_fusion.1
  151.8 1.5 cholesky.18
  153.3 0.6 compare_reduce_fusion
  153.9 0.6 select_bitcast_fusion
  154.6 1.2 custom-call.24
  155.8 0.8 copy.18
  156.6 0.8 reshape_reshape.3
  157.4 0.2 copy.20
  157.6 0.4 fusion.31
  157.9 0.2 fusion.28
  158.3 0.7 multiply_reduce_fusion.1
  159.2 55.1 %all-gather.4.cloned.1.call-done = bf16[1024,8192]{1,0:T(8,128)(2,1)} async-done(((bf16[16,8192]{1,0:T(8,128)(2,1)}), bf16[1024,8192]{1,0:T(8,128)(2,1)}) %all-gather.4.cloned.1.call-update) | async-done | bytes 16777232 | tf_op jit(solution)/shard_map/all_gather | solution.py:41
  214.3 98.2 %while.18 = (s32[]{:T(128)}, f32[112]{0:T(128)S(1)}, f32[112]{0:T(128)S(1)}, bf16[1024,8192]{1,0:T(8,128)(2,1)}, f32[16,16]{1,0:T(8,128)S(1)}, /*index=5*/f32[10...) while((s32[]{:T(128)}, f32[112]{0:T(128)S(1)}, ...), condition=%wide.region_7.8_spmd.clone, body=%wide.region_3.7_spmd.clone.sunk | while | flops 652428992 | bytes 15458425 | solution.py:83
  214.3 2.5 fusion.67
  216.8 1.2 custom-call.29
  218.0 0.3 fusion.68
  218.5 5.4 %multiply_reduce_fusion.3 = (f32[1024]{0:T(1024)S(1)}, f32[1024,1024]{0,1:T(8,128)S(1)}) fusion(bf16[1024,8192]{1,0:T(8,128)(2,1)} %get-tuple-element.371, s32[]{:T(128)S(6)} %select_n.19, f32[16,1024]{1,0:T(8,128)S(1)} %fusion.69, f32[1024,16]{0,1:T(8,128)S(1)} %get-tuple-element.373), kind=kOutput, calls=%fused_computation.1.clone.1 | convolution fusion | flops 205519872 | bytes 6426628 | tf_op jit(solution)/shard_map/while/body/eval_jaxpr/dot_general | solution.py:65
  223.9 2.6 fusion.70
  226.5 2.5 fusion.67
  229.1 1.2 custom-call.29
  230.3 0.3 fusion.68
  230.8 5.4 %multiply_reduce_fusion.3 = (f32[1024]{0:T(1024)S(1)}, f32[1024,1024]{0,1:T(8,128)S(1)}) fusion(bf16[1024,8192]{1,0:T(8,128)(2,1)} %get-tuple-element.371, s32[]{:T(128)S(6)} %select_n.19, f32[16,1024]{1,0:T(8,128)S(1)} %fusion.69, f32[1024,16]{0,1:T(8,128)S(1)} %get-tuple-element.373), kind=kOutput, calls=%fused_computation.1.clone.1 | convolution fusion | flops 205519872 | bytes 6426628 | tf_op jit(solution)/shard_map/while/body/eval_jaxpr/dot_general | solution.py:65
  236.2 2.6 fusion.70
  238.8 2.5 fusion.67
  241.4 1.2 custom-call.29
  242.6 0.3 fusion.68
  242.9 0.2 fusion.69
  243.1 5.4 %multiply_reduce_fusion.3 = (f32[1024]{0:T(1024)S(1)}, f32[1024,1024]{0,1:T(8,128)S(1)}) fusion(bf16[1024,8192]{1,0:T(8,128)(2,1)} %get-tuple-element.371, s32[]{:T(128)S(6)} %select_n.19, f32[16,1024]{1,0:T(8,128)S(1)} %fusion.69, f32[1024,16]{0,1:T(8,128)S(1)} %get-tuple-element.373), kind=kOutput, calls=%fused_computation.1.clone.1 | convolution fusion | flops 205519872 | bytes 6426628 | tf_op jit(solution)/shard_map/while/body/eval_jaxpr/dot_general | solution.py:65
  248.5 2.6 fusion.70
  251.1 2.5 fusion.67
  253.6 1.2 custom-call.29
  254.9 0.3 fusion.68
  255.3 5.4 %multiply_reduce_fusion.3 = (f32[1024]{0:T(1024)S(1)}, f32[1024,1024]{0,1:T(8,128)S(1)}) fusion(bf16[1024,8192]{1,0:T(8,128)(2,1)} %get-tuple-element.371, s32[]{:T(128)S(6)} %select_n.19, f32[16,1024]{1,0:T(8,128)S(1)} %fusion.69, f32[1024,16]{0,1:T(8,128)S(1)} %get-tuple-element.373), kind=kOutput, calls=%fused_computation.1.clone.1 | convolution fusion | flops 205519872 | bytes 6426628 | tf_op jit(solution)/shard_map/while/body/eval_jaxpr/dot_general | solution.py:65
  260.8 2.6 fusion.70
  263.4 2.5 fusion.67
  265.9 1.2 custom-call.29
  267.2 0.3 fusion.68
  267.4 0.2 fusion.69
  267.6 5.4 %multiply_reduce_fusion.3 = (f32[1024]{0:T(1024)S(1)}, f32[1024,1024]{0,1:T(8,128)S(1)}) fusion(bf16[1024,8192]{1,0:T(8,128)(2,1)} %get-tuple-element.371, s32[]{:T(128)S(6)} %select_n.19, f32[16,1024]{1,0:T(8,128)S(1)} %fusion.69, f32[1024,16]{0,1:T(8,128)S(1)} %get-tuple-element.373), kind=kOutput, calls=%fused_computation.1.clone.1 | convolution fusion | flops 205519872 | bytes 6426628 | tf_op jit(solution)/shard_map/while/body/eval_jaxpr/dot_general | solution.py:65
  273.1 2.6 fusion.70
  275.7 2.5 fusion.67
  278.2 1.2 custom-call.29
  279.4 0.3 fusion.68
  279.9 5.4 %multiply_reduce_fusion.3 = (f32[1024]{0:T(1024)S(1)}, f32[1024,1024]{0,1:T(8,128)S(1)}) fusion(bf16[1024,8192]{1,0:T(8,128)(2,1)} %get-tuple-element.371, s32[]{:T(128)S(6)} %select_n.19, f32[16,1024]{1,0:T(8,128)S(1)} %fusion.69, f32[1024,16]{0,1:T(8,128)S(1)} %get-tuple-element.373), kind=kOutput, calls=%fused_computation.1.clone.1 | convolution fusion | flops 205519872 | bytes 6426628 | tf_op jit(solution)/shard_map/while/body/eval_jaxpr/dot_general | solution.py:65
  285.4 2.6 fusion.70
  288.0 2.5 fusion.67
  290.5 1.2 custom-call.29
  291.7 0.3 fusion.68
  292.0 0.2 fusion.69
  292.2 5.4 %multiply_reduce_fusion.3 = (f32[1024]{0:T(1024)S(1)}, f32[1024,1024]{0,1:T(8,128)S(1)}) fusion(bf16[1024,8192]{1,0:T(8,128)(2,1)} %get-tuple-element.371, s32[]{:T(128)S(6)} %select_n.19, f32[16,1024]{1,0:T(8,128)S(1)} %fusion.69, f32[1024,16]{0,1:T(8,128)S(1)} %get-tuple-element.373), kind=kOutput, calls=%fused_computation.1.clone.1 | convolution fusion | flops 205519872 | bytes 6426628 | tf_op jit(solution)/shard_map/while/body/eval_jaxpr/dot_general | solution.py:65
  297.6 2.6 fusion.70
  300.2 2.5 fusion.67
  302.8 1.2 custom-call.29
  304.0 0.3 fusion.68
  304.5 5.4 %multiply_reduce_fusion.3 = (f32[1024]{0:T(1024)S(1)}, f32[1024,1024]{0,1:T(8,128)S(1)}) fusion(bf16[1024,8192]{1,0:T(8,128)(2,1)} %get-tuple-element.371, s32[]{:T(128)S(6)} %select_n.19, f32[16,1024]{1,0:T(8,128)S(1)} %fusion.69, f32[1024,16]{0,1:T(8,128)S(1)} %get-tuple-element.373), kind=kOutput, calls=%fused_computation.1.clone.1 | convolution fusion | flops 205519872 | bytes 6426628 | tf_op jit(solution)/shard_map/while/body/eval_jaxpr/dot_general | solution.py:65
  309.9 2.6 fusion.70
  312.5 0.5 broadcast_multiply_fusion
  (39 shorter events, 1.7 us)
Async XLA Ops:
  7.2 207.1 %all-gather.4.cloned.1.call-start = ((), (), s32[]{:S(2)}) async-start(), calls=%async_computation.1 | async-start | bytes 17039360 | tf_op jit(solution)/shard_map/all_gather | solution.py:41
  10.4 147.0 %all-to-all-start = ((f32[16,64,112]{2,0,1:T(8,128)}), f32[16,64,112]{2,0,1:T(8,128)S(1)}, u32[]{:S(2)}, u32[]{:S(2)}) async-start(f32[16,64,112]{2,0,1:T(8,128)} %copy.19), calls=%async_computation | async-start | bytes 1048576 | tf_op jit(solution)/shard_map/all_to_all | solution.py:42
Sparse Core Ops, SparseCore 0:
  9.9 204.3 all-gather.3
where the time goes:
time: 321 us; the launch traced here: 320 us
  blocking collectives  106 us (33%)
  matrix products  89.5 us (28%)
  waiting for transfers between devices  55.8 us (17%)
  starting transfers between devices  34.4 us (11%)
  other arithmetic  14.6 us (5%)
  between operations  14.1 us (4%)
  local copies, waits for them, and re-layouts  4.66 us (1%)
    all_gather x2, blocking collectives, gather_in_order(): parts = lax.all_gather(parts, axes[k])  106 us
    all_gather x1, waiting for transfers between devices, local(): dose_all = lax.all_gather(dosage, TILE, axis=0, tiled=True)  55.1 us
    dot_general x8, matrix products, one_block(): jnp.dot(covars_all, beta_dose, precision=highest, preferred_element_type=...  43.4 us
    all_to_all x1, starting transfers between devices, local(): lax.all_to_all(phenotypes, TILE, split_axis=1, concat_axis=0, tiled=True)  34.3 us
    dot_general x8, matrix products, one_block(): lax.dot_general(pheno_bf, dose_resid.astype(jnp.bfloat16), (((0,), (0,)),...  20.5 us
    dot_general x8, matrix products, one_block(): jnp.dot(covars_all.T, dose_block, precision=highest, preferred_element_ty...  20.1 us
    another operation x16, other arithmetic, one_block(): beta_dose = jax.scipy.linalg.cho_solve((factor, True), cov_dose)  9.88 us
  transfers between devices with their start and end apart: 2, of which 1 were waited for; matrix products, arithmetic and copies ran while one was open for 3% of the time, Pallas kernels for 0%

commit v1 on v0

--- a/solution.py
+++ b/solution.py
@@ -38,7 +38,9 @@
     gene_own = genes_all // devices
     scale_root = jnp.sqrt(jnp.float32(samples))
     covars_all = whole_of(covars, TILE, (0, 1), 0)
-    dose_all = lax.all_gather(dosage, TILE, axis=0, tiled=True)
+    dose_all = jnp.concatenate(
+        lax.all_to_all(jnp.stack([dosage] * lax.axis_size(TILE)), TILE, 0, 0), axis=0
+    )
     pheno_own = lax.all_to_all(phenotypes, TILE, split_axis=1, concat_axis=0, tiled=True)
     gram = jnp.dot(covars_all.T, covars_all, precision=highest, preferred_element_type=jnp.float32)
     factor = jnp.linalg.cholesky(gram)

time: 321 us -> 1720 us (5.36)
  blocking collectives: 106 us -> 1590 us
  waiting for transfers between devices: 55.8 us -> 0.01 us
  starting transfers between devices: 34.4 us -> 7.53 us
    all_gather x2, blocking collectives: 106 us -> 1500 us  [gather_in_order(): parts = lax.all_gather(parts, axes[k])]
    all_to_all x0 -> x1, blocking collectives: none -> 98.1 us  [local(): lax.all_to_all(phenotypes, TILE, split_axis=1, concat_axis=0, tiled=True)]
    all_gather x1 -> x0, waiting for transfers between devices: 55.1 us -> none  [local(): dose_all = lax.all_gather(dosage, TILE, axis=0, tiled=True)]
    all_to_all x1, starting transfers between devices: 34.3 us -> 7.53 us  [local(): lax.all_to_all(jnp.stack([dosage] * lax.axis_size(TILE)), TILE, 0, 0)]
  transfers between devices with their start and end apart: 2 -> 1, of which waited for: 1 -> 0; matrix products, arithmetic and copies ran while one was open for 3% -> 0% of each run, Pallas kernels for 0% -> 0%
where the time goes in v1:
time: 1720 us
  blocking collectives  1590 us (92%)
  matrix products  89.6 us (5%)
    all_gather x2, blocking collectives, gather_in_order(): parts = lax.all_gather(parts, axes[k])  1500 us
    all_to_all x1, blocking collectives, local(): lax.all_to_all(phenotypes, TILE, split_axis=1, concat_axis=0, tiled=True)  98.1 us
    dot_general x8, matrix products, one_block(): jnp.dot(covars_all, beta_dose, precision=highest, preferred_element_type=...  43.4 us
  transfers between devices with their start and end apart: 1, of which 0 were waited for; matrix products, arithmetic and copies ran while one was open for 0% of the time, Pallas kernels for 0%

profile of v1, /device:TPU:37, one launch (start us, length us, event | category | flops | bytes accessed | tf_op | source)
XLA Modules:
  0.0 1717.4 jit_solution(7346706548844746509)
XLA Ops:
  0.6 1.3 all_to_all.18
  2.0 0.3 copy.19
  2.3 98.1 %all_to_all.24 = f32[16,64,112]{2,0,1:T(8,128)S(1)} all-to-all(f32[16,64,112]{2,0,1:T(8,128)S(1)} %copy.19), channel_id=1, replica_groups=mesh['cohort'=4,'tile_0'=32,'tile_1'=2] {'tile_0','tile_1'}, dimensions={1} | all-to-all | bytes 917504 | tf_op jit(solution)/shard_map/all_to_all | solution.py:44
  100.4 6.7 stack.2
  107.1 7.5 all-to-all-start
  114.6 1480.3 %all-gather = f32[512,16]{1,0:T(8,128)S(1)} all-gather(f32[16,16]{1,0:T(8,128)S(1)} %copy-done), channel_id=2, replica_groups=mesh['cohort'=4,'tile_0'=32,'tile_1'=2] {'tile_0'}, dimensions={0}, use_global_device_ids=true | all-gather | bytes 33792 | tf_op jit(solution)/shard_map/all_gather | solution.py:20
  1594.9 15.5 all-gather.1
  1610.4 0.2 copy.16
  1610.7 0.5 convolution_bitcast_fusion.1
  1611.2 1.5 cholesky.18
  1612.7 0.8 copy.18
  1613.5 0.8 reshape_reshape.3
  1614.3 0.6 compare_reduce_fusion
  1614.9 0.6 select_bitcast_fusion
  1615.6 1.2 custom-call.24
  1616.8 0.2 copy.20
  1617.0 0.4 fusion.31
  1617.4 0.2 fusion.28
  1617.7 0.7 multiply_reduce_fusion.1
  1618.6 98.3 %while.18 = (s32[]{:T(128)}, f32[112]{0:T(128)S(1)}, f32[112]{0:T(128)S(1)}, bf16[1024,8192]{1,0:T(8,128)(2,1)}, f32[16,16]{1,0:T(8,128)S(1)}, /*index=5*/f32[10...) while((s32[]{:T(128)}, f32[112]{0:T(128)S(1)}, ...), condition=%wide.region_7.8_spmd.clone, body=%wide.region_3.7_spmd.clone.sunk | while | flops 652428992 | bytes 15458433 | solution.py:85
  1618.6 2.5 fusion.67
  1621.2 1.2 custom-call.29
  1622.4 0.3 fusion.68
  1622.9 5.4 multiply_reduce_fusion.3
  1628.3 2.6 fusion.70
  1630.9 2.5 fusion.67
  1633.4 1.2 custom-call.29
  1634.7 0.3 fusion.68
  1634.9 0.2 fusion.69
  1635.1 5.4 multiply_reduce_fusion.3
  1640.6 2.6 fusion.70
  1643.2 2.5 fusion.67
  1645.7 1.2 custom-call.29
  1647.0 0.3 fusion.68
  1647.2 0.2 fusion.69
  1647.4 5.4 multiply_reduce_fusion.3
  1652.9 2.6 fusion.70
  1655.5 2.5 fusion.67
  1658.0 1.2 custom-call.29
  1659.2 0.3 fusion.68
  1659.5 0.2 fusion.69
  1659.7 5.4 multiply_reduce_fusion.3
  1665.2 2.6 fusion.70
  1667.8 2.5 fusion.67
  1670.3 1.2 custom-call.29
  1671.5 0.3 fusion.68
  1672.0 5.4 multiply_reduce_fusion.3
  1677.4 2.6 fusion.70
  1680.0 2.5 fusion.67
  1682.6 1.2 custom-call.29
  1683.8 0.3 fusion.68
  1684.3 5.4 multiply_reduce_fusion.3
  1689.7 2.6 fusion.70
  1692.3 2.5 fusion.67
  1694.9 1.2 custom-call.29
  1696.1 0.3 fusion.68
  1696.6 5.4 multiply_reduce_fusion.3
  1702.0 2.6 fusion.70
  1704.6 2.5 fusion.67
  1707.2 1.2 custom-call.29
  1708.4 0.3 fusion.68
  1708.9 5.4 multiply_reduce_fusion.3
  1714.3 2.6 fusion.70
  1716.9 0.5 broadcast_multiply_fusion
  (40 shorter events, 1.6 us)
Async XLA Ops:
  107.1 7.6 copy-start
  107.1 1511.5 %all-to-all-start = ((bf16[64,16,8192]{2,1,0:T(8,128)(2,1)}), bf16[64,16,8192]{2,1,0:T(8,128)(2,1)}, u32[]{:S(2)}, u32[]{:S(2)}) async-start(bf16[64,16,8192]{2,1,0:T(8,128)(2,1)} %stack.2), calls=%async_computation | async-start | bytes 33554432 | tf_op jit(solution)/shard_map/all_to_all | solution.py:42
